TPU v7x, 16 devices: a whole 2x2x2 slice. The times are simulated.
16 devices in a mesh: ty: 4 (over z, y), tx: 4 (over x, core).
Axes of the slice: x: 2, y: 2, z: 2, core: 2. Of those that a mesh axis runs over, the one named last changes fastest.
Arguments:
- w_in: float32 [4, 4, 4, 384, 1536], P('tx', 'ty')
- w_out: float32 [4, 4, 4, 1536, 384], P('tx', 'ty')
- inputs: bfloat16 [4, 4, 4, 4096, 384], P('tx', 'ty')
- targets: bfloat16 [4, 4, 4, 4096, 384], P('tx', 'ty')
Outputs:
- output 1: float32 [4, 4, 4, 384, 1536], P('tx', 'ty')
- output 2: float32 [4, 4, 4, 1536, 384], P('tx', 'ty')
- output 3: float32 [4, 4, 4, 384, 1536], P('tx', 'ty')
- output 4: float32 [4, 4, 4, 1536, 384], P('tx', 'ty')
All inputs are finite; a program needn't handle non-finite values.
Results may differ from a plain program's by a relative error of at most 0.00533436.
Values are sent between devices in bfloat16 or wider.
A program may use at most 1 GiB of HBM per device.

v0:
```python
import jax
import jax.numpy as jnp
from jax import lax
from jax.sharding import PartitionSpec as P

EPS = 1e-6
LEARN_RATE = 0.125


def layer_step(hidden, mat_in, mat_out):
    hidden_f32 = hidden.astype(jnp.float32)
    inv_rms = lax.rsqrt(jnp.mean(hidden_f32 * hidden_f32, axis=-1, keepdims=True) + EPS)
    normed = (hidden_f32 * inv_rms).astype(jnp.bfloat16)
    pre_act = jnp.dot(normed, mat_in.astype(jnp.bfloat16), preferred_element_type=jnp.float32)
    gelu_out = jax.nn.gelu(pre_act).astype(jnp.bfloat16)
    mlp_out = jnp.dot(gelu_out, mat_out.astype(jnp.bfloat16), preferred_element_type=jnp.float32)
    return (hidden_f32 + mlp_out).astype(jnp.bfloat16)


def local_loss(w_in, w_out, batch_in, batch_tgt):
    hidden = batch_in
    for layer_idx in range(w_in.shape[0]):
        hidden = layer_step(hidden, w_in[layer_idx], w_out[layer_idx])
    resid_err = hidden.astype(jnp.float32) - batch_tgt.astype(jnp.float32)
    return jnp.mean(resid_err * resid_err)


local_grads = jax.grad(local_loss, argnums=(0, 1))


def neighbour_shift(values, axis_name, axis_size, offset):
    perm_pairs = [(source, (source + offset) % axis_size) for source in range(axis_size)]
    return lax.ppermute(values, axis_name, perm_pairs)


def solution(mesh):
    size_x = mesh.shape['tx']
    size_y = mesh.shape['ty']

    def gossip_mix(values):
        sent_copy = values.astype(jnp.bfloat16)
        from_xm = neighbour_shift(sent_copy, 'tx', size_x, 1)
        from_xp = neighbour_shift(sent_copy, 'tx', size_x, -1)
        from_ym = neighbour_shift(sent_copy, 'ty', size_y, 1)
        from_yp = neighbour_shift(sent_copy, 'ty', size_y, -1)
        summed = values + from_xm.astype(jnp.float32)
        summed = summed + from_xp.astype(jnp.float32)
        summed = summed + from_ym.astype(jnp.float32)
        summed = summed + from_yp.astype(jnp.float32)
        return summed / 5.0

    def device_fn(w_in, w_out, inputs, targets):
        p_in = w_in[0, 0]
        p_out = w_out[0, 0]
        batch_in = inputs[0, 0]
        batch_tgt = targets[0, 0]
        step_size = LEARN_RATE
        grad_in, grad_out = local_grads(p_in, p_out, batch_in[0], batch_tgt[0])
        y_in, y_out = grad_in, grad_out
        for step_idx in range(1, batch_in.shape[0]):
            p_in = gossip_mix(p_in) - step_size * y_in
            p_out = gossip_mix(p_out) - step_size * y_out
            mixed_yin = gossip_mix(y_in)
            mixed_yout = gossip_mix(y_out)
            new_gin, new_gout = local_grads(p_in, p_out, batch_in[step_idx], batch_tgt[step_idx])
            y_in = mixed_yin + new_gin - grad_in
            y_out = mixed_yout + new_gout - grad_out
            grad_in, grad_out = new_gin, new_gout
        return p_in[None, None], p_out[None, None], y_in[None, None], y_out[None, None]

    block_spec = P('tx', 'ty')
    return jax.shard_map(device_fn, mesh=mesh, in_specs=(block_spec, block_spec, block_spec, block_spec), out_specs=(block_spec, block_spec, block_spec, block_spec), check_vma=False)
```

profile of v0, /device:TPU:0, one launch (start us, length us, event | category | flops | bytes accessed | tf_op | source)
XLA Modules:
  0.0 2944.1 jit_solution(14693353411617871089)
XLA Ops:
  341.6 29.2 fusion.416
  464.6 42.4 %collective-permute-done.2 = bf16[4,384,1536]{2,1,0:T(8,128)(2,1)} collective-permute-done((bf16[4,384,1536]{2,1,0:T(8,128)(2,1)}, bf16[4,384,1536]{2,1,0:T(8,128)(2,1)}, u32[]{:S(2)}, u32[]{:S(2)}) %collective-permute-start.2) | collective-permute-done | bytes 4718624 | tf_op jit(solution)/shard_map/ppermute | solution.py:33
  508.1 100.5 %collective-permute-done.3 = bf16[4,384,1536]{2,1,0:T(8,128)(2,1)} collective-permute-done((bf16[4,384,1536]{2,1,0:T(8,128)(2,1)}, bf16[4,384,1536]{2,1,0:T(8,128)(2,1)}, u32[]{:S(2)}, u32[]{:S(2)}) %collective-permute-start.3) | collective-permute-done | bytes 4718624 | tf_op jit(solution)/shard_map/ppermute | solution.py:33
  794.1 26.6 fusion.23
  831.4 26.3 fusion.27
  899.7 28.8 fusion.421
  930.3 41.7 %collective-permute-done.10 = bf16[4,384,1536]{2,1,0:T(8,128)(2,1)} collective-permute-done((bf16[4,384,1536]{2,1,0:T(8,128)(2,1)}, bf16[4,384,1536]{2,1,0:T(8,128)(2,1)}, u32[]{:S(2)}, u32[]{:S(2)}) %collective-permute-start.10) | collective-permute-done | bytes 4718624 | tf_op jit(solution)/shard_map/ppermute | solution.py:33
  972.0 99.7 %collective-permute-done.11 = bf16[4,384,1536]{2,1,0:T(8,128)(2,1)} collective-permute-done((bf16[4,384,1536]{2,1,0:T(8,128)(2,1)}, bf16[4,384,1536]{2,1,0:T(8,128)(2,1)}, u32[]{:S(2)}, u32[]{:S(2)}) %collective-permute-start.11) | collective-permute-done | bytes 4718624 | tf_op jit(solution)/shard_map/ppermute | solution.py:33
  1104.8 69.4 %collective-permute-done.6 = bf16[4,384,1536]{2,1,0:T(8,128)(2,1)} collective-permute-done((bf16[4,384,1536]{2,1,0:T(8,128)(2,1)}, bf16[4,384,1536]{2,1,0:T(8,128)(2,1)}, u32[]{:S(2)}, u32[]{:S(2)}) %collective-permute-start.6) | collective-permute-done | bytes 4718624 | tf_op jit(solution)/shard_map/ppermute | solution.py:33
  1174.2 97.6 %collective-permute-done.7 = bf16[4,384,1536]{2,1,0:T(8,128)(2,1)} collective-permute-done((bf16[4,384,1536]{2,1,0:T(8,128)(2,1)}, bf16[4,384,1536]{2,1,0:T(8,128)(2,1)}, u32[]{:S(2)}, u32[]{:S(2)}) %collective-permute-start.7) | collective-permute-done | bytes 4718624 | tf_op jit(solution)/shard_map/ppermute | solution.py:33
  1322.9 54.5 %collective-permute-done.26 = bf16[4,1536,384]{2,1,0:T(8,128)(2,1)} collective-permute-done((bf16[4,1536,384]{2,1,0:T(8,128)(2,1)}, bf16[4,1536,384]{2,1,0:T(8,128)(2,1)}, u32[]{:S(2)}, u32[]{:S(2)}) %collective-permute-start.26) | collective-permute-done | bytes 4718624 | tf_op jit(solution)/shard_map/ppermute | solution.py:33
  1378.0 100.3 %collective-permute-done.27 = bf16[4,1536,384]{2,1,0:T(8,128)(2,1)} collective-permute-done((bf16[4,1536,384]{2,1,0:T(8,128)(2,1)}, bf16[4,1536,384]{2,1,0:T(8,128)(2,1)}, u32[]{:S(2)}, u32[]{:S(2)}) %collective-permute-start.27) | collective-permute-done | bytes 4718624 | tf_op jit(solution)/shard_map/ppermute | solution.py:33
  1775.7 29.2 fusion.426
  1810.6 66.4 %collective-permute-done.21 = bf16[4,384,1536]{2,1,0:T(8,128)(2,1)} collective-permute-done((bf16[4,384,1536]{2,1,0:T(8,128)(2,1)}, bf16[4,384,1536]{2,1,0:T(8,128)(2,1)}, u32[]{:S(2)}, u32[]{:S(2)}) %collective-permute-start.21) | collective-permute-done | bytes 4718624 | tf_op jit(solution)/shard_map/ppermute | solution.py:33
  1917.8 63.1 %collective-permute-done.23 = bf16[4,384,1536]{2,1,0:T(8,128)(2,1)} collective-permute-done((bf16[4,384,1536]{2,1,0:T(8,128)(2,1)}, bf16[4,384,1536]{2,1,0:T(8,128)(2,1)}, u32[]{:S(2)}, u32[]{:S(2)}) %collective-permute-start.23) | collective-permute-done | bytes 4718624 | tf_op jit(solution)/shard_map/ppermute | solution.py:33
  1983.2 99.5 %collective-permute-done.18 = bf16[4,384,1536]{2,1,0:T(8,128)(2,1)} collective-permute-done((bf16[4,384,1536]{2,1,0:T(8,128)(2,1)}, bf16[4,384,1536]{2,1,0:T(8,128)(2,1)}, u32[]{:S(2)}, u32[]{:S(2)}) %collective-permute-start.18) | collective-permute-done | bytes 4718624 | tf_op jit(solution)/shard_map/ppermute | solution.py:33
  2082.7 100.5 %collective-permute-done.19 = bf16[4,384,1536]{2,1,0:T(8,128)(2,1)} collective-permute-done((bf16[4,384,1536]{2,1,0:T(8,128)(2,1)}, bf16[4,384,1536]{2,1,0:T(8,128)(2,1)}, u32[]{:S(2)}, u32[]{:S(2)}) %collective-permute-start.19) | collective-permute-done | bytes 4718624 | tf_op jit(solution)/shard_map/ppermute | solution.py:33
  2183.2 28.2 fusion.526
  2234.4 50.5 %collective-permute-done.34 = bf16[4,1536,384]{2,1,0:T(8,128)(2,1)} collective-permute-done((bf16[4,1536,384]{2,1,0:T(8,128)(2,1)}, bf16[4,1536,384]{2,1,0:T(8,128)(2,1)}, u32[]{:S(2)}, u32[]{:S(2)}) %collective-permute-start.34) | collective-permute-done | bytes 4718624 | tf_op jit(solution)/shard_map/ppermute | solution.py:33
  2284.9 100.5 %collective-permute-done.35 = bf16[4,1536,384]{2,1,0:T(8,128)(2,1)} collective-permute-done((bf16[4,1536,384]{2,1,0:T(8,128)(2,1)}, bf16[4,1536,384]{2,1,0:T(8,128)(2,1)}, u32[]{:S(2)}, u32[]{:S(2)}) %collective-permute-start.35) | collective-permute-done | bytes 4718624 | tf_op jit(solution)/shard_map/ppermute | solution.py:33
  2603.2 27.4 fusion.63
  2654.9 29.0 fusion.431
  2775.7 54.0 %collective-permute-done.42 = bf16[4,384,1536]{2,1,0:T(8,128)(2,1)} collective-permute-done((bf16[4,384,1536]{2,1,0:T(8,128)(2,1)}, bf16[4,384,1536]{2,1,0:T(8,128)(2,1)}, u32[]{:S(2)}, u32[]{:S(2)}) %collective-permute-start.42) | collective-permute-done | bytes 4718624 | tf_op jit(solution)/shard_map/ppermute | solution.py:33
  2829.7 100.8 %collective-permute-done.43 = bf16[4,384,1536]{2,1,0:T(8,128)(2,1)} collective-permute-done((bf16[4,384,1536]{2,1,0:T(8,128)(2,1)}, bf16[4,384,1536]{2,1,0:T(8,128)(2,1)}, u32[]{:S(2)}, u32[]{:S(2)}) %collective-permute-start.43) | collective-permute-done | bytes 4718624 | tf_op jit(solution)/shard_map/ppermute | solution.py:33
  (583 shorter events, 1475.3 us)
Async XLA Ops:
  12.0 387.6 %collective-permute-start.12 = (bf16[4,1536,384]{2,1,0:T(8,128)(2,1)}, bf16[4,1536,384]{2,1,0:T(8,128)(2,1)}, u32[]{:S(2)}, u32[]{:S(2)}) collective-permute-start(bf16[4,1536,384]{2,1,0:T(8,128)(2,1)} %get-tuple-element.30), channel_id=1, source_target_pairs={{0,1},{1,2},{2,3},{3,0},{4,5},{5,6},{6,7},{7,4},{8,9},{9,10},{10,1... | collective-permute-start | bytes 14155784 | tf_op jit(solution)/shard_map/ppermute | solution.py:33
  12.8 388.6 %collective-permute-start.13 = (bf16[4,1536,384]{2,1,0:T(8,128)(2,1)}, bf16[4,1536,384]{2,1,0:T(8,128)(2,1)}, u32[]{:S(2)}, u32[]{:S(2)}) collective-permute-start(bf16[4,1536,384]{2,1,0:T(8,128)(2,1)} %get-tuple-element.30), channel_id=1, source_target_pairs={{0,3},{1,0},{2,1},{3,2},{4,7},{5,4},{6,5},{7,6},{8,11},{9,8},{10,9... | collective-permute-start | bytes 14155784 | tf_op jit(solution)/shard_map/ppermute | solution.py:33
  14.7 387.7 %collective-permute-start.14 = (bf16[4,1536,384]{2,1,0:T(8,128)(2,1)}, bf16[4,1536,384]{2,1,0:T(8,128)(2,1)}, u32[]{:S(2)}, u32[]{:S(2)}) collective-permute-start(bf16[4,1536,384]{2,1,0:T(8,128)(2,1)} %get-tuple-element.30), channel_id=1, source_target_pairs={{0,4},{4,8},{8,12},{12,0},{1,5},{5,9},{9,13},{13,1},{2,6},{6,10},{... | collective-permute-start | bytes 14155784 | tf_op jit(solution)/shard_map/ppermute | solution.py:33
  17.0 407.7 %collective-permute-start.15 = (bf16[4,1536,384]{2,1,0:T(8,128)(2,1)}, bf16[4,1536,384]{2,1,0:T(8,128)(2,1)}, u32[]{:S(2)}, u32[]{:S(2)}) collective-permute-start(bf16[4,1536,384]{2,1,0:T(8,128)(2,1)} %get-tuple-element.30), channel_id=1, source_target_pairs={{0,12},{4,0},{8,4},{12,8},{1,13},{5,1},{9,5},{13,9},{2,14},{6,2},{... | collective-permute-start | bytes 14155784 | tf_op jit(solution)/shard_map/ppermute | solution.py:33
  22.7 418.3 %collective-permute-start = (bf16[4,384,1536]{2,1,0:T(8,128)(2,1)}, bf16[4,384,1536]{2,1,0:T(8,128)(2,1)}, u32[]{:S(2)}, u32[]{:S(2)}) collective-permute-start(bf16[4,384,1536]{2,1,0:T(8,128)(2,1)} %get-tuple-element.32), channel_id=1, source_target_pairs={{0,1},{1,2},{2,3},{3,0},{4,5},{5,6},{6,7},{7,4},{8,9},{9,10},{10,1... | collective-permute-start | bytes 14155784 | tf_op jit(solution)/shard_map/ppermute | solution.py:33
  440.9 456.4 %collective-permute-start.28 = (bf16[4,1536,384]{2,1,0:T(8,128)(2,1)}, bf16[4,1536,384]{2,1,0:T(8,128)(2,1)}, u32[]{:S(2)}, u32[]{:S(2)}) collective-permute-start(bf16[4,1536,384]{2,1,0:T(8,128)(2,1)} %get-tuple-element.34), channel_id=1, source_target_pairs={{0,1},{1,2},{2,3},{3,0},{4,5},{5,6},{6,7},{7,4},{8,9},{9,10},{10,1... | collective-permute-start | bytes 14155784 | tf_op jit(solution)/shard_map/ppermute | solution.py:33
  440.9 458.7 %collective-permute-start.29 = (bf16[4,1536,384]{2,1,0:T(8,128)(2,1)}, bf16[4,1536,384]{2,1,0:T(8,128)(2,1)}, u32[]{:S(2)}, u32[]{:S(2)}) collective-permute-start(bf16[4,1536,384]{2,1,0:T(8,128)(2,1)} %get-tuple-element.34), channel_id=1, source_target_pairs={{0,3},{1,0},{2,1},{3,2},{4,7},{5,4},{6,5},{7,6},{8,11},{9,8},{10,9... | collective-permute-start | bytes 14155784 | tf_op jit(solution)/shard_map/ppermute | solution.py:33
  462.7 465.8 %collective-permute-start.30 = (bf16[4,1536,384]{2,1,0:T(8,128)(2,1)}, bf16[4,1536,384]{2,1,0:T(8,128)(2,1)}, u32[]{:S(2)}, u32[]{:S(2)}) collective-permute-start(bf16[4,1536,384]{2,1,0:T(8,128)(2,1)} %get-tuple-element.34), channel_id=1, source_target_pairs={{0,4},{4,8},{8,12},{12,0},{1,5},{5,9},{9,13},{13,1},{2,6},{6,10},{... | collective-permute-start | bytes 14155784 | tf_op jit(solution)/shard_map/ppermute | solution.py:33
  507.0 423.3 %collective-permute-start.31 = (bf16[4,1536,384]{2,1,0:T(8,128)(2,1)}, bf16[4,1536,384]{2,1,0:T(8,128)(2,1)}, u32[]{:S(2)}, u32[]{:S(2)}) collective-permute-start(bf16[4,1536,384]{2,1,0:T(8,128)(2,1)} %get-tuple-element.34), channel_id=1, source_target_pairs={{0,12},{4,0},{8,4},{12,8},{1,13},{5,1},{9,5},{13,9},{2,14},{6,2},{... | collective-permute-start | bytes 14155784 | tf_op jit(solution)/shard_map/ppermute | solution.py:33
  930.3 243.9 %collective-permute-start.6 = (bf16[4,384,1536]{2,1,0:T(8,128)(2,1)}, bf16[4,384,1536]{2,1,0:T(8,128)(2,1)}, u32[]{:S(2)}, u32[]{:S(2)}) collective-permute-start(bf16[4,384,1536]{2,1,0:T(8,128)(2,1)} %get-tuple-element.20), channel_id=1, source_target_pairs={{0,4},{4,8},{8,12},{12,0},{1,5},{5,9},{9,13},{13,1},{2,6},{6,10},{... | collective-permute-start | bytes 14155784 | tf_op jit(solution)/shard_map/ppermute | solution.py:33
  972.0 299.8 %collective-permute-start.7 = (bf16[4,384,1536]{2,1,0:T(8,128)(2,1)}, bf16[4,384,1536]{2,1,0:T(8,128)(2,1)}, u32[]{:S(2)}, u32[]{:S(2)}) collective-permute-start(bf16[4,384,1536]{2,1,0:T(8,128)(2,1)} %get-tuple-element.20), channel_id=1, source_target_pairs={{0,12},{4,0},{8,4},{12,8},{1,13},{5,1},{9,5},{13,9},{2,14},{6,2},{... | collective-permute-start | bytes 14155784 | tf_op jit(solution)/shard_map/ppermute | solution.py:33
  1274.7 498.4 %collective-permute-start.36 = (bf16[4,1536,384]{2,1,0:T(8,128)(2,1)}, bf16[4,1536,384]{2,1,0:T(8,128)(2,1)}, u32[]{:S(2)}, u32[]{:S(2)}) collective-permute-start(bf16[4,1536,384]{2,1,0:T(8,128)(2,1)} %get-tuple-element.11), channel_id=1, source_target_pairs={{0,1},{1,2},{2,3},{3,0},{4,5},{5,6},{6,7},{7,4},{8,9},{9,10},{10,1... | collective-permute-start | bytes 14155784 | tf_op jit(solution)/shard_map/ppermute | solution.py:33
  1321.2 453.7 %collective-permute-start.37 = (bf16[4,1536,384]{2,1,0:T(8,128)(2,1)}, bf16[4,1536,384]{2,1,0:T(8,128)(2,1)}, u32[]{:S(2)}, u32[]{:S(2)}) collective-permute-start(bf16[4,1536,384]{2,1,0:T(8,128)(2,1)} %get-tuple-element.11), channel_id=1, source_target_pairs={{0,3},{1,0},{2,1},{3,2},{4,7},{5,4},{6,5},{7,6},{8,11},{9,8},{10,9... | collective-permute-start | bytes 14155784 | tf_op jit(solution)/shard_map/ppermute | solution.py:33
  1322.9 482.1 %collective-permute-start.38 = (bf16[4,1536,384]{2,1,0:T(8,128)(2,1)}, bf16[4,1536,384]{2,1,0:T(8,128)(2,1)}, u32[]{:S(2)}, u32[]{:S(2)}) collective-permute-start(bf16[4,1536,384]{2,1,0:T(8,128)(2,1)} %get-tuple-element.11), channel_id=1, source_target_pairs={{0,4},{4,8},{8,12},{12,0},{1,5},{5,9},{9,13},{13,1},{2,6},{6,10},{... | collective-permute-start | bytes 14155784 | tf_op jit(solution)/shard_map/ppermute | solution.py:33
  1377.4 429.7 %collective-permute-start.39 = (bf16[4,1536,384]{2,1,0:T(8,128)(2,1)}, bf16[4,1536,384]{2,1,0:T(8,128)(2,1)}, u32[]{:S(2)}, u32[]{:S(2)}) collective-permute-start(bf16[4,1536,384]{2,1,0:T(8,128)(2,1)} %get-tuple-element.11), channel_id=1, source_target_pairs={{0,12},{4,0},{8,4},{12,8},{1,13},{5,1},{9,5},{13,9},{2,14},{6,2},{... | collective-permute-start | bytes 14155784 | tf_op jit(solution)/shard_map/ppermute | solution.py:33
  1880.5 302.7 %collective-permute-start.19 = (bf16[4,384,1536]{2,1,0:T(8,128)(2,1)}, bf16[4,384,1536]{2,1,0:T(8,128)(2,1)}, u32[]{:S(2)}, u32[]{:S(2)}) collective-permute-start(bf16[4,384,1536]{2,1,0:T(8,128)(2,1)} %get-tuple-element.15), channel_id=1, source_target_pairs={{0,12},{4,0},{8,4},{12,8},{1,13},{5,1},{9,5},{13,9},{2,14},{6,2},{... | collective-permute-start | bytes 14155784 | tf_op jit(solution)/shard_map/ppermute | solution.py:33
  1981.0 251.3 %collective-permute-start.32 = (bf16[4,1536,384]{2,1,0:T(8,128)(2,1)}, bf16[4,1536,384]{2,1,0:T(8,128)(2,1)}, u32[]{:S(2)}, u32[]{:S(2)}) collective-permute-start(bf16[4,1536,384]{2,1,0:T(8,128)(2,1)} %get-tuple-element.13), channel_id=1, source_target_pairs={{0,1},{1,2},{2,3},{3,0},{4,5},{5,6},{6,7},{7,4},{8,9},{9,10},{10,1... | collective-permute-start | bytes 14155784 | tf_op jit(solution)/shard_map/ppermute | solution.py:33
  1981.0 253.0 %collective-permute-start.33 = (bf16[4,1536,384]{2,1,0:T(8,128)(2,1)}, bf16[4,1536,384]{2,1,0:T(8,128)(2,1)}, u32[]{:S(2)}, u32[]{:S(2)}) collective-permute-start(bf16[4,1536,384]{2,1,0:T(8,128)(2,1)} %get-tuple-element.13), channel_id=1, source_target_pairs={{0,3},{1,0},{2,1},{3,2},{4,7},{5,4},{6,5},{7,6},{8,11},{9,8},{10,9... | collective-permute-start | bytes 14155784 | tf_op jit(solution)/shard_map/ppermute | solution.py:33
  1982.7 302.2 %collective-permute-start.34 = (bf16[4,1536,384]{2,1,0:T(8,128)(2,1)}, bf16[4,1536,384]{2,1,0:T(8,128)(2,1)}, u32[]{:S(2)}, u32[]{:S(2)}) collective-permute-start(bf16[4,1536,384]{2,1,0:T(8,128)(2,1)} %get-tuple-element.13), channel_id=1, source_target_pairs={{0,4},{4,8},{8,12},{12,0},{1,5},{5,9},{9,13},{13,1},{2,6},{6,10},{... | collective-permute-start | bytes 14155784 | tf_op jit(solution)/shard_map/ppermute | solution.py:33
  2082.7 302.7 %collective-permute-start.35 = (bf16[4,1536,384]{2,1,0:T(8,128)(2,1)}, bf16[4,1536,384]{2,1,0:T(8,128)(2,1)}, u32[]{:S(2)}, u32[]{:S(2)}) collective-permute-start(bf16[4,1536,384]{2,1,0:T(8,128)(2,1)} %get-tuple-element.13), channel_id=1, source_target_pairs={{0,12},{4,0},{8,4},{12,8},{1,13},{5,1},{9,5},{13,9},{2,14},{6,2},{... | collective-permute-start | bytes 14155784 | tf_op jit(solution)/shard_map/ppermute | solution.py:33
  2183.2 539.1 %collective-permute-start.44 = (bf16[4,1536,384]{2,1,0:T(8,128)(2,1)}, bf16[4,1536,384]{2,1,0:T(8,128)(2,1)}, u32[]{:S(2)}, u32[]{:S(2)}) collective-permute-start(bf16[4,1536,384]{2,1,0:T(8,128)(2,1)} %get-tuple-element.4), channel_id=1, source_target_pairs={{0,1},{1,2},{2,3},{3,0},{4,5},{5,6},{6,7},{7,4},{8,9},{9,10},{10,1... | collective-permute-start | bytes 14155784 | tf_op jit(solution)/shard_map/ppermute | solution.py:33
  2232.2 491.9 %collective-permute-start.45 = (bf16[4,1536,384]{2,1,0:T(8,128)(2,1)}, bf16[4,1536,384]{2,1,0:T(8,128)(2,1)}, u32[]{:S(2)}, u32[]{:S(2)}) collective-permute-start(bf16[4,1536,384]{2,1,0:T(8,128)(2,1)} %get-tuple-element.4), channel_id=1, source_target_pairs={{0,3},{1,0},{2,1},{3,2},{4,7},{5,4},{6,5},{7,6},{8,11},{9,8},{10,9... | collective-permute-start | bytes 14155784 | tf_op jit(solution)/shard_map/ppermute | solution.py:33
  2234.0 490.6 %collective-permute-start.46 = (bf16[4,1536,384]{2,1,0:T(8,128)(2,1)}, bf16[4,1536,384]{2,1,0:T(8,128)(2,1)}, u32[]{:S(2)}, u32[]{:S(2)}) collective-permute-start(bf16[4,1536,384]{2,1,0:T(8,128)(2,1)} %get-tuple-element.4), channel_id=1, source_target_pairs={{0,4},{4,8},{8,12},{12,0},{1,5},{5,9},{9,13},{13,1},{2,6},{6,10},{... | collective-permute-start | bytes 14155784 | tf_op jit(solution)/shard_map/ppermute | solution.py:33
  2284.9 462.4 %collective-permute-start.47 = (bf16[4,1536,384]{2,1,0:T(8,128)(2,1)}, bf16[4,1536,384]{2,1,0:T(8,128)(2,1)}, u32[]{:S(2)}, u32[]{:S(2)}) collective-permute-start(bf16[4,1536,384]{2,1,0:T(8,128)(2,1)} %get-tuple-element.4), channel_id=1, source_target_pairs={{0,12},{4,0},{8,4},{12,8},{1,13},{5,1},{9,5},{13,9},{2,14},{6,2},{... | collective-permute-start | bytes 14155784 | tf_op jit(solution)/shard_map/ppermute | solution.py:33
  (192 other events, 10073.1 us)
where the time goes:
time: 2950 us; the launch traced here: 2940 us
  matrix products  1330 us (45%)
  waiting for transfers between devices  1280 us (43%)
  other arithmetic  246 us (8%)
  local copies, waits for them, and re-layouts  43.4 us (1%)
  starting transfers between devices  42.5 us (1%)
    ppermute x48, waiting for transfers between devices, neighbour_shift(): return lax.ppermute(values, axis_name, perm_pairs)  1280 us
    dot_general x44, matrix products, layer_step(): jnp.dot(normed, mat_in.astype(jnp.bfloat16), preferred_element_type=jnp.f...  674 us
    dot_general x44, matrix products, layer_step(): jnp.dot(gelu_out, mat_out.astype(jnp.bfloat16), preferred_element_type=jn...  654 us
    convert_element_type x8, other arithmetic, gossip_mix(): sent_copy = values.astype(jnp.bfloat16)  90.7 us
    another operation x4, other arithmetic  77.1 us
  transfers between devices with their start and end apart: 48, of which 20 were waited for; matrix products, arithmetic and copies ran while one was open for 54% of the time, Pallas kernels for 0%

commit v1 on v0

v1 whole, which is shorter than its diff:
```python
import functools

import jax
import jax.numpy as jnp
import numpy as np
from jax import lax
from jax.experimental import pallas as pl
from jax.experimental.pallas import tpu as pltpu
from jax.sharding import PartitionSpec as P

bf16, f32 = jnp.bfloat16, jnp.float32
EPS = 1e-6
LEARN_RATE = 0.125
GELU_A = float(np.sqrt(2 / np.pi))
GELU_B = GELU_A * 0.044715
TILE = 512
COLS = 768
SUB = 96
CORE, XDIR, YDIR, ZDIR = range(4)


def dot_nt(a, b):
    return lax.dot_general(a, b, (((1,), (1,)), ((), ())), preferred_element_type=f32)


def dot_nn(a, b):
    return jnp.dot(a, b, preferred_element_type=f32)


def step_kernel(step, last, names, *refs):
    r = dict(zip(names, refs))
    first = step == 0
    x_ref, t_ref, nb, w, dw = r['x'], r['t'], r['nb'], r['w'], r['dw']
    mats, d, ff = w.shape
    rows = x_ref.shape[1]
    tiles = rows // TILE
    subs = d // SUB
    chunks = mats * subs
    send_sem, recv_sem = r['send_sem'], r['recv_sem']
    sets = nb.shape[0]
    p_set = None if last else sets - 1
    y_set = None if first else 0

    tx, ty = lax.axis_index('tx'), lax.axis_index('ty')
    peers = (
        {'tx': tx + 1 - 2 * lax.rem(tx, 2)},
        {'tx': 3 - tx},
        {'ty': ty + 1 - 2 * lax.rem(ty, 2)},
        {'ty': lax.rem(ty + 2, 4)},
    )
    xpar, ypar = lax.rem(tx, 2), lax.rem(ty, 2)
    order = (1 - xpar, xpar, 3 - ypar, 2 + ypar)

    def remote(src, group, direction, mat):
        slot = group * mats + mat
        return pltpu.make_async_remote_copy(
            src_ref=src, dst_ref=nb.at[group, direction, mat],
            send_sem=send_sem.at[direction, slot], recv_sem=recv_sem.at[direction, slot],
            device_id=peers[direction], device_id_type=pl.DeviceIdType.MESH)

    def send(src, group, mat):
        for direction in (YDIR, XDIR, CORE):
            remote(src.at[mat], group, direction, mat).start()

    def arrived(group, direction, mat):
        remote(nb.at[group, direction, mat], group, direction, mat).wait_recv()

    def forward(slot):
        group, mat = lax.div(slot, mats), lax.rem(slot, mats)
        arrived(group, YDIR, mat)
        remote(nb.at[group, YDIR, mat], group, ZDIR, mat).start()

    def where(q):
        return lax.div(q, subs), pl.ds(pl.multiple_of(lax.rem(q, subs) * SUB, SUB), SUB)

    def stream(ins, outs, body, before=None):
        def get(q, slot):
            mat, rng = where(q)
            return [pltpu.make_async_copy(src(mat, rng), buf.at[slot], r['in_sem'].at[k, slot])
                    for k, (src, buf) in enumerate(ins)]

        def put(q, slot):
            mat, rng = where(q)
            return [pltpu.make_async_copy(buf.at[slot], dst(mat, rng), r['out_sem'].at[k, slot])
                    for k, (buf, dst) in enumerate(outs)]

        if before is not None:
            before(0)
        for c in get(0, 0):
            c.start()

        def one(q, carry):
            slot = lax.rem(q, 2)

            @pl.when(q + 1 < chunks)
            def _():
                if before is not None:
                    @pl.when(lax.rem(q + 1, subs) == 0)
                    def _():
                        before(lax.div(q + 1, subs))
                for c in get(q + 1, 1 - slot):
                    c.start()
            for c in get(q, slot):
                c.wait()

            @pl.when(q >= 2)
            def _():
                for c in put(q - 2, slot):
                    c.wait()
            body(q, slot)
            for c in put(q, slot):
                c.start()
            return carry

        lax.fori_loop(0, chunks, one, 0)
        for q in (chunks - 2, chunks - 1):
            for c in put(q, q % 2):
                c.wait()

    def mix(v, bn, slot):
        for k in range(4):
            v = v + bn[k, slot].astype(f32)
        return v / 5.0

    def neighbour(source, group, k):
        return lambda mat, rng: source.at[group, order[k], mat, rng]

    if not first:
        def send_y(mat, carry):
            send(r['y_send'], y_set, mat)
            return carry
        lax.fori_loop(0, mats, send_y, 0)

    def late_send(q):
        if p_set is not None:
            @pl.when(jnp.logical_and(lax.rem(q, subs) == 0, q > 0))
            def _():
                send(w, p_set, lax.div(q, subs) - 1)

    if first:
        def load_weights(bp):
            def body(q, slot):
                mat, rng = where(q)
                w[mat, rng, :] = bp[slot].astype(bf16)
                late_send(q)
            stream([(lambda mat, rng: r['p'].at[mat, rng], bp)], [], body)
        pl.run_scoped(load_weights, pltpu.VMEM((2, SUB, ff), f32))
    else:
        def new_weights(bp, bn, by, bo):
            def body(q, slot):
                mat, rng = where(q)
                pn = mix(bp[slot], bn, slot) - LEARN_RATE * by[slot].astype(f32)
                bo[slot] = pn
                w[mat, rng, :] = pn.astype(bf16)
                late_send(q)
            pnb = r['p_nb']
            ins = [(lambda mat, rng: r['p'].at[mat, rng], bp)]
            ins += [(neighbour(pnb, pnb.shape[0] - 1, k), bn.at[k]) for k in range(4)]
            ins += [(lambda mat, rng: r['y'].at[mat, rng], by)]
            stream(ins, [(bo, lambda mat, rng: r['p_out'].at[mat, rng])], body)
        pl.run_scoped(new_weights, pltpu.VMEM((2, SUB, ff), f32), pltpu.VMEM((4, 2, SUB, ff), bf16),
                      pltpu.VMEM((2, SUB, ff), r['y'].dtype), pltpu.VMEM((2, SUB, ff), f32))

    def zero(k, carry):
        dw[lax.div(k, subs), where(k)[1], :] = jnp.zeros((SUB, ff), f32)
        return carry
    lax.fori_loop(0, chunks, zero, 0)
    if p_set is not None:
        send(w, p_set, mats - 1)

    layers = mats // 2
    inv_count = 1.0 / (rows * d)

    def gradient(xb, tb, h_s, a_s, gp_s, dh_s):
        def fetch(i, slot):
            rng = pl.ds(pl.multiple_of(i * TILE, TILE), TILE)
            return (pltpu.make_async_copy(x_ref.at[step, rng], xb.at[slot], r['tile_sem'].at[0, slot]),
                    pltpu.make_async_copy(t_ref.at[step, rng], tb.at[slot], r['tile_sem'].at[1, slot]))
        for c in fetch(0, 0):
            c.start()

        def tile(i, carry):
            slot = lax.rem(i, 2)
            if first:
                @pl.when(i > 0)
                def _():
                    forward(i - 1)
            else:
                forward(i)
            for c in fetch(i, slot):
                c.wait()

            @pl.when(i + 1 < tiles)
            def _():
                for c in fetch(i + 1, 1 - slot):
                    c.start()
            h_s[0] = xb[slot]

            def fwd(l, carry):
                h = h_s[l].astype(f32)
                inv = lax.rsqrt(jnp.mean(h * h, axis=-1, keepdims=True) + EPS)
                u = (h * inv).astype(bf16)
                acc = jnp.zeros((TILE, d), f32)
                for c in range(0, ff, COLS):
                    cs = slice(c, c + COLS)
                    z = dot_nn(u, w[2 * l, :, cs])
                    z2 = z * z
                    th = jnp.tanh(z * (GELU_A + GELU_B * z2))
                    s = 0.5 + 0.5 * th
                    a = (z * s).astype(bf16)
                    a_s[l, :, cs] = a
                    gp_s[l, :, cs] = s + (z * (0.5 * GELU_A + 1.5 * GELU_B * z2)) * (1.0 - th * th)
                    acc = acc + dot_nt(a, w[2 * l + 1, :, cs])
                h_s[l + 1] = (h + acc).astype(bf16)
                return carry
            lax.fori_loop(0, layers, fwd, 0)

            err = h_s[layers].astype(f32) - tb[slot].astype(f32)
            dh_s[...] = ((err * inv_count) * 2.0).astype(bf16)

            def bwd(l, bottom):
                g = dh_s[...]
                g_t = g.T
                h = h_s[l].astype(f32)
                inv = lax.rsqrt(jnp.mean(h * h, axis=-1, keepdims=True) + EPS)
                u_t = (h * inv).astype(bf16).T
                du = jnp.zeros((TILE, d), f32)
                for c in range(0, ff, COLS):
                    cs = slice(c, c + COLS)
                    da = dot_nn(g, w[2 * l + 1, :, cs]).astype(bf16).astype(f32)
                    dz = (da * gp_s[l, :, cs]).astype(bf16)
                    dw[2 * l, :, cs] += dot_nn(u_t, dz)
                    dw[2 * l + 1, :, cs] += dot_nn(g_t, a_s[l, :, cs])
                    if not bottom:
                        du = du + dot_nt(dz, w[2 * l, :, cs])
                if not bottom:
                    du = du.astype(bf16).astype(f32)
                    dinv = jnp.sum(du * h, axis=-1, keepdims=True)
                    k = dinv * (inv * inv * inv) * (-1.0 / d)
                    dh_s[...] = (g.astype(f32) + du * inv + h * k).astype(bf16)

            def bwd_down(q, carry):
                bwd(layers - 1 - q, False)
                return carry
            lax.fori_loop(0, layers - 1, bwd_down, 0)
            bwd(0, True)
            return carry

        lax.fori_loop(0, tiles, tile, 0)

    pl.run_scoped(gradient, pltpu.VMEM((2, TILE, d), bf16), pltpu.VMEM((2, TILE, d), bf16),
                  pltpu.VMEM((layers + 1, TILE, d), bf16), pltpu.VMEM((layers, TILE, ff), bf16),
                  pltpu.VMEM((layers, TILE, ff), f32), pltpu.VMEM((TILE, d), bf16))

    sent = tiles - 1 if first else tiles
    slots = sets * mats
    if first:
        forward(sent)

        def new_tracker(og):
            def body(q, slot):
                mat, rng = where(q)
                og[slot] = dw[mat, rng, :].astype(bf16)
            stream([], [(og, lambda mat, rng: r['g_out'].at[mat, rng])], body)
        pl.run_scoped(new_tracker, pltpu.VMEM((2, SUB, ff), bf16))
    else:
        if not last:
            forward(sent)
            sent += 1
        same = 'g' not in r

        def new_tracker(bn, by, bg, bo, ob, og):
            def before(mat):
                for direction in (CORE, XDIR, ZDIR):
                    arrived(y_set, direction, mat)
                if not last:
                    @pl.when(mat == mats // 2)
                    def _():
                        forward(tiles + 1)

            def body(q, slot):
                mat, rng = where(q)
                g = dw[mat, rng, :].astype(bf16)
                old = (by if same else bg)[slot].astype(f32)
                y = (mix(by[slot].astype(f32), bn, slot) + g.astype(f32)) - old
                bo[slot] = y
                if not last:
                    ob[slot] = y.astype(bf16)
                    og[slot] = g
            ins = [(lambda mat, rng: r['y'].at[mat, rng], by)]
            ins += [(neighbour(nb, y_set, k), bn.at[k]) for k in range(4)]
            if not same:
                ins += [(lambda mat, rng: r['g'].at[mat, rng], bg)]
            outs = [(bo, lambda mat, rng: r['y_out'].at[mat, rng])]
            if not last:
                outs += [(ob, lambda mat, rng: r['yb_out'].at[mat, rng]),
                         (og, lambda mat, rng: r['g_out'].at[mat, rng])]
            stream(ins, outs, body, before)
        block = (2, SUB, ff)
        pl.run_scoped(new_tracker, pltpu.VMEM((4,) + block, bf16), pltpu.VMEM(block, r['y'].dtype), pltpu.VMEM(block, bf16),
                      pltpu.VMEM(block, f32), pltpu.VMEM(block, bf16), pltpu.VMEM(block, bf16))
        if not last:
            sent += 1

    if first:
        sent += 1

    def rest(slot, carry):
        forward(slot)
        return carry
    lax.fori_loop(sent, slots, rest, 0)

    def drain(slot, carry):
        group, mat = lax.div(slot, mats), lax.rem(slot, mats)
        for direction in range(4):
            remote(nb.at[group, direction, mat], group, direction, mat).wait_send()
        return carry
    lax.fori_loop(0, slots, drain, 0)
    if p_set is not None:
        def settle(mat, carry):
            for direction in (CORE, XDIR, ZDIR):
                arrived(p_set, direction, mat)
            return carry
        lax.fori_loop(0, mats, settle, 0)


def run_step(step, last, ins):
    mats, d, ff = ins['p'].shape
    first = step == 0
    sets = 1 if first or last else 2
    big = lambda dtype: jax.ShapeDtypeStruct((mats, d, ff), dtype)
    outs = {'nb': jax.ShapeDtypeStruct((sets, 4, mats, d, ff), bf16)}
    if first:
        outs['g_out'] = big(bf16)
    else:
        outs['p_out'] = big(f32)
        outs['y_out'] = big(f32)
        if not last:
            outs['yb_out'] = big(bf16)
            outs['g_out'] = big(bf16)
    scratch = {
        'w': pltpu.VMEM((mats, d, ff), bf16),
        'dw': pltpu.VMEM((mats, d, ff), f32),
        'send_sem': pltpu.SemaphoreType.DMA((4, sets * mats)),
        'recv_sem': pltpu.SemaphoreType.DMA((4, sets * mats)),
        'in_sem': pltpu.SemaphoreType.DMA((6, 2)),
        'out_sem': pltpu.SemaphoreType.DMA((3, 2)),
        'tile_sem': pltpu.SemaphoreType.DMA((2, 2)),
    }
    names = tuple(ins) + tuple(outs) + tuple(scratch)
    anywhere = pl.BlockSpec(memory_space=pl.ANY)
    res = pl.pallas_call(
        functools.partial(step_kernel, step, last, names),
        out_shape=tuple(outs.values()),
        in_specs=[anywhere] * len(ins),
        out_specs=tuple(anywhere for _ in outs),
        scratch_shapes=list(scratch.values()),
        compiler_params=pltpu.CompilerParams(vmem_limit_bytes=67043328, has_side_effects=True),
        name='step%d' % step,
    )(*ins.values())
    return dict(zip(outs, res))


def solution(mesh):
    def device_fn(w_in, w_out, inputs, targets):
        layers, d, ff = w_in.shape[2:]
        x, t = inputs[0, 0], targets[0, 0]
        steps = x.shape[0] - 1
        p = jnp.stack([w_in[0, 0], jnp.swapaxes(w_out[0, 0], 1, 2)], axis=1).reshape(2 * layers, d, ff)
        out = run_step(0, False, {'x': x, 't': t, 'p': p})
        y, y_send, g, p_nb = out['g_out'], out['g_out'], None, out['nb']
        for step in range(1, steps + 1):
            ins = {'x': x, 't': t, 'p': p, 'p_nb': p_nb, 'y': y}
            if g is None:
                ins['y_send'] = y_send
            else:
                ins['y_send'] = y_send
                ins['g'] = g
            out = run_step(step, step == steps, ins)
            p, y, p_nb = out['p_out'], out['y_out'], out['nb']
            if step < steps:
                y_send, g = out['yb_out'], out['g_out']

        def split(v):
            v = v.reshape(layers, 2, d, ff)
            return v[:, 0][None, None], jnp.swapaxes(v[:, 1], 1, 2)[None, None]
        return split(p) + split(y)

    spec = P('tx', 'ty')
    return jax.shard_map(device_fn, mesh=mesh, in_specs=(spec,) * 4, out_specs=(spec,) * 4, check_vma=False)
```

time: 2950 us -> 1530 us (0.52)
  Pallas kernels: 0 us -> 1420 us
  matrix products: 1330 us -> 0 us
  waiting for transfers between devices: 1280 us -> 0 us
  other arithmetic: 246 us -> 14.5 us
  starting transfers between devices: 42.5 us -> 0 us
  local copies, waits for them, and re-layouts: 43.4 us -> 75 us
    pallas_call x0 -> x4, Pallas kernels: none -> 1420 us  [run_step(): pl.pallas_call(functools.partial(step_kernel, step, last, names), out_sha...]
    dot_general x88 -> x0, matrix products: 1330 us -> none  [the longest x44 674 us: layer_step(): jnp.dot(normed, mat_in.astype(jnp.bfloat16), preferred_element_type=jnp.f...]
    ppermute x48 -> x0, waiting for transfers between devices: 1280 us -> none  [neighbour_shift(): return lax.ppermute(values, axis_name, perm_pairs)]
    convert_element_type x20 -> x0, other arithmetic: 131 us -> none  [the longest x8 90.7 us: gossip_mix(): sent_copy = values.astype(jnp.bfloat16)]
    another operation x4 -> x1, other arithmetic: 77.1 us -> 14.5 us  [device_fn(): jnp.stack([w_in[0, 0], jnp.swapaxes(w_out[0, 0], 1, 2)], axis=1)]
    ppermute x48 -> x0, starting transfers between devices: 42.5 us -> none  [neighbour_shift(): return lax.ppermute(values, axis_name, perm_pairs)]
  transfers between devices with their start and end apart: 48 -> 0, of which waited for: 20 -> 0; matrix products, arithmetic and copies ran while one was open for 54% -> 0% of each run, Pallas kernels for 0% -> 0%
where the time goes in v1:
time: 1530 us; the launch traced here: 1510 us
  Pallas kernels  1420 us (93%)
  local copies, waits for them, and re-layouts  75 us (5%)
    pallas_call x4, Pallas kernels, run_step(): pl.pallas_call(functools.partial(step_kernel, step, last, names), out_sha...  1420 us

profile of v1, /device:TPU:0, one launch (start us, length us, event | category | flops | bytes accessed | tf_op | source)
XLA Modules:
  0.0 1514.6 jit_solution(1274178547349276768)
XLA Ops:
  0.6 9.6 copy.8
  10.2 14.5 pad_maximum_fusion
  24.7 19.0 %copy.9 = f32[4,2,384,1536]{3,2,1,0:T(8,128)} copy(f32[4,2,384,1536]{2,3,0,1:T(8,128)} %pad_maximum_fusion) | data formatting | bytes 37748736 | tf_op jit(solution)/shard_map/stack | solution.py:369
  43.7 254.0 %step0.1 = (bf16[1,4,8,384,1536]{4,3,2,1,0:T(8,128)(2,1)}, bf16[8,384,1536]{2,1,0:T(8,128)(2,1)}) custom-call(bf16[4,4096,384]{2,1,0:T(8,128)(2,1)} %bitcast.29, bf16[4,4096,384]{2,1,0:T(8,128)(2,1)} %bitcast.33, f32[8,384,1536]{2,1,0:T(8,128)} %bitcast.37), custom_call_target="tpu_custom_call" | custom-call | tf_op jit(solution)/shard_map/step0/pallas_call | solution.py:352
  297.7 450.2 %step1.1 = (bf16[2,4,8,384,1536]{4,3,2,1,0:T(8,128)(2,1)}, f32[8,384,1536]{2,1,0:T(8,128)}, f32[8,384,1536]{2,1,0:T(8,128)}, bf16[8,384,1536]{2,1,0:T(8,128)(2,1)}, bf16[8,384,1536]{2,1,0:T(8,128)(2,1)}) custom-call(bf16[4,4096,384]{2,1,0:T(8,128)(2,1)} %bitcast.30, bf16[4,4096,384]{2,1,0:T(8,128)(2,1)} %bitcast.34, f32[8,384,1536]{2,1,0:T(8,128)} %bitcast.38, ...), custom_call_target="tpu_custom_call" | custom-call | tf_op jit(solution)/shard_map/step1/pallas_call | solution.py:352
  747.9 452.0 %step2.1 = (bf16[2,4,8,384,1536]{4,3,2,1,0:T(8,128)(2,1)}, f32[8,384,1536]{2,1,0:T(8,128)}, f32[8,384,1536]{2,1,0:T(8,128)}, bf16[8,384,1536]{2,1,0:T(8,128)(2,1)}, bf16[8,384,1536]{2,1,0:T(8,128)(2,1)}) custom-call(bf16[4,4096,384]{2,1,0:T(8,128)(2,1)} %bitcast.31, bf16[4,4096,384]{2,1,0:T(8,128)(2,1)} %bitcast.35, ...), custom_call_target="tpu_custom_call" | custom-call | tf_op jit(solution)/shard_map/step2/pallas_call | solution.py:352
  1199.8 267.9 %step3.1 = (bf16[1,4,8,384,1536]{4,3,2,1,0:T(8,128)(2,1)}, f32[8,384,1536]{2,1,0:T(8,128)}, f32[8,384,1536]{2,1,0:T(8,128)}) custom-call(bf16[4,4096,384]{2,1,0:T(8,128)(2,1)} %bitcast.32, bf16[4,4096,384]{2,1,0:T(8,128)(2,1)} %bitcast.36, f32[8,384,1536]{2,1,0:T(8,128)} %get-tuple-element.25.refs_2_, ...), custom_call_target="tpu_custom_call" | custom-call | tf_op jit(solution)/shard_map/step3/pallas_call | solution.py:352
  1467.7 27.2 %fusion = (f32[4,1,384,1536]{3,2,1,0:T(8,128)}, f32[1,1,4,384,1536]{4,3,2,1,0:T(8,128)}, f32[1,1,4,384,1536]{4,3,2,1,0:T(8,128)}, f32[4,1,384,1536]{3,2,1,0:T(8,128)}) fusion(f32[4,2,384,1536]{3,2,1,0:T(8,128)} %bitcast.41, f32[4,2,384,1536]{3,2,1,0:T(8,128)} %bitcast.40), kind=kLoop, calls=%fused_computation.3 | loop fusion | bytes 75497472 | tf_op jit(solution)/shard_map/slice | solution.py:386
  1495.0 9.6 copy.17
  1504.6 9.6 copy.15

commit v2 on v0

v2 whole, which is shorter than its diff:
```python
import functools

import jax
import jax.numpy as jnp
import numpy as np
from jax import lax
from jax.experimental import pallas as pl
from jax.experimental.pallas import tpu as pltpu
from jax.sharding import PartitionSpec as P

bf16, f32 = jnp.bfloat16, jnp.float32
EPS = 1e-6
LEARN_RATE = 0.125
GELU_A = float(np.sqrt(2 / np.pi))
GELU_B = GELU_A * 0.044715
TILE = 512
COLS = 768
SUB = 128
DEPTH = 4
PARTS = 2
CORE, XDIR, YDIR, ZDIR = range(4)


def dot_nt(a, b):
    return lax.dot_general(a, b, (((1,), (1,)), ((), ())), preferred_element_type=f32)


def dot_nn(a, b):
    return jnp.dot(a, b, preferred_element_type=f32)


def where(q, subs):
    return lax.div(q, subs), pl.ds(pl.multiple_of(lax.rem(q, subs) * SUB, SUB), SUB)


class Block:
    def __init__(self, hbm, buf, sem, incoming):
        self.hbm, self.buf, self.sem, self.incoming = hbm, buf, sem, incoming

    def run(self, mat, rng, slot, act):
        hbm, buf, sem = self.hbm(mat, rng), self.buf.at[slot], self.sem.at[slot]
        pair = (hbm, buf) if self.incoming else (buf, hbm)
        act(pltpu.make_async_copy(*pair, sem))


class SplitBlock:
    def __init__(self, w_in, w_out, buf, buf_t, sem, incoming):
        self.w_in, self.w_out, self.buf, self.buf_t, self.sem, self.incoming = w_in, w_out, buf, buf_t, sem, incoming

    def run(self, mat, rng, slot, act):
        layer, odd = lax.div(mat, 2), lax.rem(mat, 2)

        def go(hbm, buf):
            pair = (hbm, buf) if self.incoming else (buf, hbm)
            act(pltpu.make_async_copy(*pair, self.sem.at[slot]))

        @pl.when(odd == 0)
        def _():
            go(self.w_in.at[layer, rng], self.buf.at[slot])

        @pl.when(odd == 1)
        def _():
            go(self.w_out.at[layer, :, rng], self.buf_t.at[slot])

    def take(self, mat, slot):
        @pl.when(lax.rem(mat, 2) == 1)
        def _():
            self.buf[slot] = self.buf_t[slot].T

    def give(self, mat, slot, value):
        @pl.when(lax.rem(mat, 2) == 0)
        def _():
            self.buf[slot] = value

        @pl.when(lax.rem(mat, 2) == 1)
        def _():
            self.buf_t[slot] = value.T


def stream(mats, subs, ins, outs, body, before=None):
    chunks = mats * subs

    def get(q):
        if before is not None:
            @pl.when(lax.rem(q, subs) == 0)
            def _():
                before(lax.div(q, subs))
        mat, rng = where(q, subs)
        for b in ins:
            b.run(mat, rng, lax.rem(q, DEPTH), lambda c: c.start())

    def put(q, act):
        mat, rng = where(q, subs)
        for b in outs:
            b.run(mat, rng, lax.rem(q, DEPTH), act)

    def early(q, carry):
        get(q)
        return carry
    lax.fori_loop(0, DEPTH - 1, early, 0)

    def one(q, carry):
        mat, rng = where(q, subs)
        slot = lax.rem(q, DEPTH)

        @pl.when(q + DEPTH - 1 < chunks)
        def _():
            get(q + DEPTH - 1)
        for b in ins:
            b.run(mat, rng, slot, lambda c: c.wait())

        @pl.when(q >= DEPTH)
        def _():
            put(q - DEPTH, lambda c: c.wait())
        body(mat, rng, slot)
        put(q, lambda c: c.start())
        return carry
    lax.fori_loop(0, chunks, one, 0)

    def late(q, carry):
        put(q, lambda c: c.wait())
        return carry
    lax.fori_loop(chunks - DEPTH, chunks, late, 0)


def neighbour_order():
    xpar, ypar = lax.rem(lax.axis_index('tx'), 2), lax.rem(lax.axis_index('ty'), 2)
    return 1 - xpar, xpar, 3 - ypar, 2 + ypar


def mix(v, bn, slot):
    for k in range(4):
        v = v + bn[k, slot].astype(f32)
    return v / 5.0


def rows_of(ref):
    return lambda mat, rng: ref.at[mat, rng]


def step_kernel(step, steps, names, *refs):
    r = dict(zip(names, refs))
    first, last, before_last = step == 0, step == steps, step == steps - 1
    x_ref, t_ref, nb, w, dw = r['x'], r['t'], r['nb'], r['w'], r['dw']
    mats, d, ff = w.shape
    rows = x_ref.shape[1]
    tiles = rows // TILE
    subs = d // SUB
    part_rows = d // PARTS
    per_set = mats * PARTS
    sems = r['copy_sem']
    send_sem, recv_sem = r['send_sem'], r['recv_sem']
    sets = nb.shape[0]
    slots = sets * per_set
    p_set = None if last else sets - 1
    y_set = None if first else 0
    order = neighbour_order()
    run = functools.partial(stream, mats, subs)
    block = (DEPTH, SUB, ff)

    tx, ty = lax.axis_index('tx'), lax.axis_index('ty')
    peers = (
        {'tx': tx + 1 - 2 * lax.rem(tx, 2)},
        {'tx': 3 - tx},
        {'ty': ty + 1 - 2 * lax.rem(ty, 2)},
        {'ty': lax.rem(ty + 2, 4)},
    )

    def remote(source, group, direction, mat, part):
        rng = pl.ds(pl.multiple_of(part * part_rows, part_rows), part_rows)
        slot = group * per_set + mat * PARTS + part
        src = nb.at[group, YDIR, mat, rng] if source is None else source.at[mat, rng]
        return pltpu.make_async_remote_copy(
            src_ref=src, dst_ref=nb.at[group, direction, mat, rng],
            send_sem=send_sem.at[direction, slot], recv_sem=recv_sem.at[direction, slot],
            device_id=peers[direction], device_id_type=pl.DeviceIdType.MESH)

    def send(source, group, mat):
        for part in range(PARTS):
            for direction in (YDIR, XDIR, CORE):
                remote(source, group, direction, mat, part).start()

    def arrived(group, mat, directions=(CORE, XDIR, ZDIR)):
        for part in range(PARTS):
            for direction in directions:
                remote(None, group, direction, mat, part).wait_recv()

    def forward(slot):
        group, rest = lax.div(slot, per_set), lax.rem(slot, per_set)
        mat, part = lax.div(rest, PARTS), lax.rem(rest, PARTS)
        remote(None, group, YDIR, mat, part).wait_recv()
        remote(None, group, ZDIR, mat, part).start()

    def loop(lo, hi, fn):
        def one(k, carry):
            fn(k)
            return carry
        lax.fori_loop(lo, hi, one, 0)

    def nb_blocks(source, group, buf):
        return [Block(lambda mat, rng, k=k: source.at[group, order[k], mat, rng], buf.at[k], sems.at[k], True)
                for k in range(4)]

    if not first:
        loop(0, mats, lambda mat: send(r['y_send'], y_set, mat))

    def late_send(mat, rng):
        if p_set is not None:
            @pl.when(jnp.logical_and(rng.start == 0, mat > 0))
            def _():
                send(w, p_set, mat - 1)

    if last:
        for mat in range(mats):
            pltpu.make_async_copy(r['pb'].at[mat], w.at[mat], sems.at[mat, 0]).start()
    elif first:
        def load_weights(bp, bt):
            src = SplitBlock(r['w_in'], r['w_out'], bp, bt, sems.at[4], True)

            def body(mat, rng, slot):
                src.take(mat, slot)
                w[mat, rng, :] = bp[slot].astype(bf16)
                late_send(mat, rng)
            run([src], [], body)
        pl.run_scoped(load_weights, pltpu.VMEM(block, f32), pltpu.VMEM((DEPTH, ff, SUB), f32))
    else:
        split = 'w_in' in r

        def new_weights(bp, bn, by, bo, bt=None):
            if split:
                src = SplitBlock(r['w_in'], r['w_out'], bp, bt, sems.at[4], True)
            else:
                src = Block(rows_of(r['p']), bp, sems.at[4], True)

            def body(mat, rng, slot):
                if split:
                    src.take(mat, slot)
                pn = mix(bp[slot], bn, slot) - LEARN_RATE * by[slot].astype(f32)
                bo[slot] = pn
                w[mat, rng, :] = pn.astype(bf16)
                late_send(mat, rng)
            ins = [src] + nb_blocks(r['p_nb'], r['p_nb'].shape[0] - 1, bn)
            ins += [Block(rows_of(r['y']), by, sems.at[5], True)]
            run(ins, [Block(rows_of(r['p_out']), bo, sems.at[6], False)], body)
        bufs = [pltpu.VMEM(block, f32), pltpu.VMEM((4,) + block, bf16), pltpu.VMEM(block, r['y'].dtype), pltpu.VMEM(block, f32)]
        if split:
            bufs.append(pltpu.VMEM((DEPTH, ff, SUB), f32))
        pl.run_scoped(new_weights, *bufs)

    def zero(k):
        mat, rng = where(k, subs)
        dw[mat, rng, :] = jnp.zeros((SUB, ff), f32)
    loop(0, mats * subs, zero)
    if p_set is not None:
        send(w, p_set, mats - 1)
    if last:
        for mat in range(mats):
            pltpu.make_async_copy(r['pb'].at[mat], w.at[mat], sems.at[mat, 0]).wait()

    layers = mats // 2
    inv_count = 1.0 / (rows * d)
    behind = 1 if first or last else 0

    def gradient(xb, tb, h_s, a_s, gp_s, dh_s):
        def fetch(i, slot):
            rng = pl.ds(pl.multiple_of(i * TILE, TILE), TILE)
            return (pltpu.make_async_copy(x_ref.at[step, rng], xb.at[slot], r['tile_sem'].at[0, slot]),
                    pltpu.make_async_copy(t_ref.at[step, rng], tb.at[slot], r['tile_sem'].at[1, slot]))
        for c in fetch(0, 0):
            c.start()

        def tile(i):
            slot = lax.rem(i, 2)
            if behind:
                @pl.when(i > 0)
                def _():
                    forward(PARTS * i - 1)
            else:
                forward(PARTS * i)
            for c in fetch(i, slot):
                c.wait()

            @pl.when(i + 1 < tiles)
            def _():
                for c in fetch(i + 1, 1 - slot):
                    c.start()
            h_s[0] = xb[slot]

            def fwd(l):
                h = h_s[l].astype(f32)
                inv = lax.rsqrt(jnp.mean(h * h, axis=-1, keepdims=True) + EPS)
                u = (h * inv).astype(bf16)
                acc = jnp.zeros((TILE, d), f32)
                for c in range(0, ff, COLS):
                    cs = slice(c, c + COLS)
                    z = dot_nn(u, w[2 * l, :, cs])
                    z2 = z * z
                    th = jnp.tanh(z * (GELU_A + GELU_B * z2))
                    s = 0.5 + 0.5 * th
                    a = (z * s).astype(bf16)
                    a_s[l, :, cs] = a
                    gp_s[l, :, cs] = s + (z * (0.5 * GELU_A + 1.5 * GELU_B * z2)) * (1.0 - th * th)
                    acc = acc + dot_nt(a, w[2 * l + 1, :, cs])
                h_s[l + 1] = (h + acc).astype(bf16)
            loop(0, layers, fwd)

            forward(PARTS * i + 1 - behind)
            err = h_s[layers].astype(f32) - tb[slot].astype(f32)
            dh_s[...] = ((err * inv_count) * 2.0).astype(bf16)

            def bwd(l, bottom):
                g = dh_s[...]
                g_t = g.T
                h = h_s[l].astype(f32)
                inv = lax.rsqrt(jnp.mean(h * h, axis=-1, keepdims=True) + EPS)
                u_t = (h * inv).astype(bf16).T
                du = jnp.zeros((TILE, d), f32)
                for c in range(0, ff, COLS):
                    cs = slice(c, c + COLS)
                    da = dot_nn(g, w[2 * l + 1, :, cs]).astype(bf16).astype(f32)
                    dz = (da * gp_s[l, :, cs]).astype(bf16)
                    dw[2 * l, :, cs] += dot_nn(u_t, dz)
                    dw[2 * l + 1, :, cs] += dot_nn(g_t, a_s[l, :, cs])
                    if not bottom:
                        du = du + dot_nt(dz, w[2 * l, :, cs])
                if not bottom:
                    du = du.astype(bf16).astype(f32)
                    dinv = jnp.sum(du * h, axis=-1, keepdims=True)
                    k = dinv * (inv * inv * inv) * (-1.0 / d)
                    dh_s[...] = (g.astype(f32) + du * inv + h * k).astype(bf16)

            loop(0, layers - 1, lambda q: bwd(layers - 1 - q, False))
            bwd(0, True)

        loop(0, tiles, tile)

    pl.run_scoped(gradient, pltpu.VMEM((2, TILE, d), bf16), pltpu.VMEM((2, TILE, d), bf16),
                  pltpu.VMEM((layers + 1, TILE, d), bf16), pltpu.VMEM((layers, TILE, ff), bf16),
                  pltpu.VMEM((layers, TILE, ff), f32), pltpu.VMEM((TILE, d), bf16))
    sent = tiles * PARTS - behind

    if first or last:
        forward(sent)
        sent += 1

        def keep_gradient(og):
            def body(mat, rng, slot):
                og[slot] = dw[mat, rng, :].astype(bf16)
            run([], [Block(rows_of(r['g_out']), og, sems.at[6], False)], body)
        pl.run_scoped(keep_gradient, pltpu.VMEM(block, bf16))
    else:
        forward(sent)
        forward(sent + 1)
        same = 'g' not in r

        def new_tracker(bn, by, bo, ob, og, bg=None):
            def before(mat):
                arrived(y_set, mat)
                for at, slot in ((3, sent + 2), (6, sent + 3)):
                    @pl.when(mat == at)
                    def _():
                        forward(slot)

            def body(mat, rng, slot):
                g = dw[mat, rng, :].astype(bf16)
                old = (by if same else bg)[slot].astype(f32)
                y = (mix(by[slot].astype(f32), bn, slot) + g.astype(f32)) - old
                bo[slot] = y
                ob[slot] = y.astype(bf16)
                og[slot] = g
            ins = [Block(rows_of(r['y']), by, sems.at[4], True)] + nb_blocks(nb, y_set, bn)
            if not same:
                ins += [Block(rows_of(r['g']), bg, sems.at[5], True)]
            outs = [Block(rows_of(r['y_out']), bo, sems.at[6], False),
                    Block(rows_of(r['yb_out']), ob, sems.at[7], False),
                    Block(rows_of(r['g_out']), og, sems.at[8], False)]
            run(ins, outs, body, before)
        bufs = [pltpu.VMEM((4,) + block, bf16), pltpu.VMEM(block, r['y'].dtype), pltpu.VMEM(block, f32),
                pltpu.VMEM(block, bf16), pltpu.VMEM(block, bf16)]
        if not same:
            bufs.append(pltpu.VMEM(block, bf16))
        pl.run_scoped(new_tracker, *bufs)
        sent += 4

    if before_last:
        def next_weights(bp, bn, by, bo, ob):
            def before(mat):
                for slot in range(PARTS):
                    nxt = p_set * per_set + (mat + 1) * PARTS + slot

                    @pl.when(jnp.logical_and(nxt >= sent, nxt < slots))
                    def _():
                        forward(nxt)
                arrived(p_set, mat)

            def body(mat, rng, slot):
                pn = mix(bp[slot], bn, slot) - LEARN_RATE * by[slot]
                bo[slot] = pn
                ob[slot] = pn.astype(bf16)
            ins = [Block(rows_of(r['p_out']), bp, sems.at[4], True)] + nb_blocks(nb, p_set, bn)
            ins += [Block(rows_of(r['y_out']), by, sems.at[5], True)]
            outs = [Block(rows_of(r['p_next']), bo, sems.at[6], False),
                    Block(rows_of(r['pb_next']), ob, sems.at[7], False)]
            run(ins, outs, body, before)
        pl.run_scoped(next_weights, pltpu.VMEM(block, f32), pltpu.VMEM((4,) + block, bf16), pltpu.VMEM(block, f32),
                      pltpu.VMEM(block, f32), pltpu.VMEM(block, bf16))
    else:
        loop(sent, slots, forward)
        loop(0, mats, lambda mat: arrived(y_set if last else p_set, mat))

    def drain(slot):
        group, rest = lax.div(slot, per_set), lax.rem(slot, per_set)
        for direction in range(4):
            remote(None, group, direction, lax.div(rest, PARTS), lax.rem(rest, PARTS)).wait_send()
    loop(0, slots, drain)


def final_kernel(p, y, nb, g_old, g, pi_out, po_out, yi_out, yo_out, bp, bn, by, bg, bh, bpo, bpt, byo, byt, sems):
    mats, d, _ = p.shape
    order = neighbour_order()
    p_dst = SplitBlock(pi_out, po_out, bpo, bpt, sems.at[8], False)
    y_dst = SplitBlock(yi_out, yo_out, byo, byt, sems.at[9], False)

    def body(mat, rng, slot):
        p_dst.give(mat, slot, bp[slot])
        new = (mix(by[slot], bn, slot) + bh[slot].astype(f32)) - bg[slot].astype(f32)
        y_dst.give(mat, slot, new)
    ins = [Block(rows_of(p), bp, sems.at[4], True), Block(rows_of(y), by, sems.at[5], True),
           Block(rows_of(g_old), bg, sems.at[6], True), Block(rows_of(g), bh, sems.at[7], True)]
    ins += [Block(lambda mat, rng, k=k: nb.at[0, order[k], mat, rng], bn.at[k], sems.at[k], True) for k in range(4)]
    stream(mats, d // SUB, ins, [p_dst, y_dst], body)


ANY = pl.BlockSpec(memory_space=pl.ANY)
VMEM_LIMIT = 67043328


def run_step(step, steps, dims, ins):
    mats, d, ff = dims
    first, last = step == 0, step == steps
    sets = 1 if first or last else 2
    big = lambda dtype: jax.ShapeDtypeStruct(dims, dtype)
    outs = {'nb': jax.ShapeDtypeStruct((sets, 4, mats, d, ff), bf16), 'g_out': big(bf16)}
    if not first and not last:
        outs.update(p_out=big(f32), y_out=big(f32), yb_out=big(bf16))
    if step == steps - 1:
        outs.update(p_next=big(f32), pb_next=big(bf16))
    scratch = {
        'w': pltpu.VMEM(dims, bf16),
        'dw': pltpu.VMEM(dims, f32),
        'send_sem': pltpu.SemaphoreType.DMA((4, sets * mats * PARTS)),
        'recv_sem': pltpu.SemaphoreType.DMA((4, sets * mats * PARTS)),
        'copy_sem': pltpu.SemaphoreType.DMA((9, DEPTH)),
        'tile_sem': pltpu.SemaphoreType.DMA((2, 2)),
    }
    names = tuple(ins) + tuple(outs) + tuple(scratch)
    res = pl.pallas_call(
        functools.partial(step_kernel, step, steps, names),
        out_shape=tuple(outs.values()),
        in_specs=[ANY] * len(ins),
        out_specs=tuple(ANY for _ in outs),
        scratch_shapes=list(scratch.values()),
        compiler_params=pltpu.CompilerParams(vmem_limit_bytes=VMEM_LIMIT, has_side_effects=True),
        name='step%d' % step,
    )(*ins.values())
    return dict(zip(outs, res))


def finish(layers, p, y, nb, g_old, g):
    mats, d, ff = p.shape
    block = (DEPTH, SUB, ff)
    block_t = (DEPTH, ff, SUB)
    w_in, w_out = jax.ShapeDtypeStruct((layers, d, ff), f32), jax.ShapeDtypeStruct((layers, ff, d), f32)
    return pl.pallas_call(
        final_kernel,
        out_shape=(w_in, w_out, w_in, w_out),
        in_specs=[ANY] * 5,
        out_specs=(ANY,) * 4,
        scratch_shapes=[pltpu.VMEM(block, f32), pltpu.VMEM((4,) + block, bf16), pltpu.VMEM(block, f32),
                        pltpu.VMEM(block, bf16), pltpu.VMEM(block, bf16),
                        pltpu.VMEM(block, f32), pltpu.VMEM(block_t, f32), pltpu.VMEM(block, f32), pltpu.VMEM(block_t, f32),
                        pltpu.SemaphoreType.DMA((10, DEPTH))],
        compiler_params=pltpu.CompilerParams(vmem_limit_bytes=VMEM_LIMIT),
        name='finish',
    )(p, y, nb, g_old, g)


def solution(mesh):
    def device_fn(w_in, w_out, inputs, targets):
        w_in, w_out = w_in[0, 0], w_out[0, 0]
        layers, d, ff = w_in.shape
        dims = (2 * layers, d, ff)
        data = {'x': inputs[0, 0], 't': targets[0, 0]}
        steps = data['x'].shape[0] - 1
        out = run_step(0, steps, dims, {**data, 'w_in': w_in, 'w_out': w_out})
        g0 = out['g_out']
        out = run_step(1, steps, dims, {**data, 'w_in': w_in, 'w_out': w_out, 'p_nb': out['nb'], 'y': g0, 'y_send': g0})
        for step in range(2, steps):
            out = run_step(step, steps, dims, {**data, 'p': out['p_out'], 'p_nb': out['nb'], 'y': out['y_out'],
                                               'y_send': out['yb_out'], 'g': out['g_out']})
        end = run_step(steps, steps, dims, {**data, 'pb': out['pb_next'], 'y_send': out['yb_out']})
        res = finish(layers, out['p_next'], out['y_out'], end['nb'], out['g_out'], end['g_out'])
        return tuple(v[None, None] for v in res)

    spec = P('tx', 'ty')
    return jax.shard_map(device_fn, mesh=mesh, in_specs=(spec,) * 4, out_specs=(spec,) * 4, check_vma=False)
```

time: 2950 us -> 1400 us (0.47)
  Pallas kernels: 0 us -> 1400 us
  matrix products: 1330 us -> 0 us
  waiting for transfers between devices: 1280 us -> 0 us
  other arithmetic: 246 us -> 0 us
  local copies, waits for them, and re-layouts: 43.4 us -> 0 us
  starting transfers between devices: 42.5 us -> 0 us
    pallas_call x0 -> x5, Pallas kernels: none -> 1400 us  [the longest x4 1350 us: run_step(): pl.pallas_call(functools.partial(step_kernel, step, steps, names), out_sh...]
    dot_general x88 -> x0, matrix products: 1330 us -> none  [the longest x44 674 us: layer_step(): jnp.dot(normed, mat_in.astype(jnp.bfloat16), preferred_element_type=jnp.f...]
    ppermute x48 -> x0, waiting for transfers between devices: 1280 us -> none  [neighbour_shift(): return lax.ppermute(values, axis_name, perm_pairs)]
    convert_element_type x20 -> x0, other arithmetic: 131 us -> none  [the longest x8 90.7 us: gossip_mix(): sent_copy = values.astype(jnp.bfloat16)]
    another operation x4 -> x0, other arithmetic: 77.1 us -> none
    ppermute x48 -> x0, starting transfers between devices: 42.5 us -> none  [neighbour_shift(): return lax.ppermute(values, axis_name, perm_pairs)]
    unnamed x344 -> x0, local copies, waits for them, and re-layouts: 31 us -> none
  transfers between devices with their start and end apart: 48 -> 0, of which waited for: 20 -> 0; matrix products, arithmetic and copies ran while one was open for 54% -> 0% of each run, Pallas kernels for 0% -> 0%
where the time goes in v2:
time: 1400 us
  Pallas kernels  1400 us (100%)
    pallas_call x4, Pallas kernels, run_step(): pl.pallas_call(functools.partial(step_kernel, step, steps, names), out_sh...  1350 us
    pallas_call x1, Pallas kernels, finish(): pl.pallas_call(final_kernel, out_shape=(w_in, w_out, w_in, w_out), in_spe...  43.2 us

profile of v2, /device:TPU:0, one launch (start us, length us, event | category | flops | bytes accessed | tf_op | source)
XLA Modules:
  0.0 1398.2 jit_solution(10246332143454999144)
XLA Ops:
  0.6 234.6 %step0.1 = (bf16[1,4,8,384,1536]{4,3,2,1,0:T(8,128)(2,1)}, bf16[8,384,1536]{2,1,0:T(8,128)(2,1)}) custom-call(bf16[4,4096,384]{2,1,0:T(8,128)(2,1)} %bitcast.8, bf16[4,4096,384]{2,1,0:T(8,128)(2,1)} %bitcast.12, f32[4,384,1536]{2,1,0:T(8,128)} %bitcast.16, f32[4,1536,384]{2,1,0:T(8,128)} %bitcast.18), custom_call_target="tpu_custom_call" | custom-call | tf_op jit(solution)/shard_map/step0/pallas_call | solution.py:457
  235.3 442.8 %step1.1 = (bf16[2,4,8,384,1536]{4,3,2,1,0:T(8,128)(2,1)}, bf16[8,384,1536]{2,1,0:T(8,128)(2,1)}, f32[8,384,1536]{2,1,0:T(8,128)}, f32[8,384,1536]{2,1,0:T(8,128)}, bf16[8,384,1536]{2,1,0:T(8,128)(2,1)}) custom-call(bf16[4,4096,384]{2,1,0:T(8,128)(2,1)} %bitcast.9, bf16[4,4096,384]{2,1,0:T(8,128)(2,1)} %bitcast.13, f32[4,384,1536]{2,1,0:T(8,128)} %bitcast.17, ...), custom_call_target="tpu_custom_call" | custom-call | tf_op jit(solution)/shard_map/step1/pallas_call | solution.py:457
  678.0 452.0 %step2.1 = (bf16[2,4,8,384,1536]{4,3,2,1,0:T(8,128)(2,1)}, bf16[8,384,1536]{2,1,0:T(8,128)(2,1)}, f32[8,384,1536]{2,1,0:T(8,128)}, f32[8,384,1536]{2,1,0:T(8,128...) custom-call(bf16[4,4096,384]{2,1,0:T(8,128)(2,1)} %bitcast.10, ...), custom_call_target="tpu_custom_call" | custom-call | tf_op jit(solution)/shard_map/step2/pallas_call | solution.py:457
  1130.0 224.5 %step3.1 = (bf16[1,4,8,384,1536]{4,3,2,1,0:T(8,128)(2,1)}, bf16[8,384,1536]{2,1,0:T(8,128)(2,1)}) custom-call(bf16[4,4096,384]{2,1,0:T(8,128)(2,1)} %bitcast.11, bf16[4,4096,384]{2,1,0:T(8,128)(2,1)} %bitcast.15, bf16[8,384,1536]{2,1,0:T(8,128)(2,1)} %get-tuple-element.31.refs_2_, bf16[8,384,1536]{2,1,0:T(8,128)(2,1)} %get-tuple-element.32.refs_3_), custom_call_target="tpu_custom_call" | custom-call | tf_op jit(solution)/shard_map/step3/pallas_call | solution.py:457
  1354.5 43.2 %finish.1 = (f32[4,384,1536]{2,1,0:T(8,128)}, f32[4,1536,384]{2,1,0:T(8,128)}, f32[4,384,1536]{2,1,0:T(8,128)}, f32[4,1536,384]{2,1,0:T(8,128)}) custom-call(f32[8,384,1536]{2,1,0:T(8,128)} %get-tuple-element.29.p, f32[8,384,1536]{2,1,0:T(8,128)} %get-tuple-element.30.y, bf16[1,4,8,384,1536]{4,3,2,1,0:T(8,128)(2,1)} %get-tuple-element.33.nb, ...), custom_call_target="tpu_custom_call" | custom-call | tf_op jit(solution)/shard_map/finish/pallas_call | solution.py:474

commit v3 on v2

--- a/solution.py
+++ b/solution.py
@@ -226,6 +226,11 @@
     else:
         split = 'w_in' in r
 
+        def first_forward(mat):
+            @pl.when(mat == 5)
+            def _():
+                forward(0)
+
         def new_weights(bp, bn, by, bo, bt=None):
             if split:
                 src = SplitBlock(r['w_in'], r['w_out'], bp, bt, sems.at[4], True)
@@ -241,7 +246,7 @@
                 late_send(mat, rng)
             ins = [src] + nb_blocks(r['p_nb'], r['p_nb'].shape[0] - 1, bn)
             ins += [Block(rows_of(r['y']), by, sems.at[5], True)]
-            run(ins, [Block(rows_of(r['p_out']), bo, sems.at[6], False)], body)
+            run(ins, [Block(rows_of(r['p_out']), bo, sems.at[6], False)], body, first_forward)
         bufs = [pltpu.VMEM(block, f32), pltpu.VMEM((4,) + block, bf16), pltpu.VMEM(block, r['y'].dtype), pltpu.VMEM(block, f32)]
         if split:
             bufs.append(pltpu.VMEM((DEPTH, ff, SUB), f32))
@@ -259,7 +264,7 @@
 
     layers = mats // 2
     inv_count = 1.0 / (rows * d)
-    behind = 1 if first or last else 0
+    behind = 1 if first or last else -1
 
     def gradient(xb, tb, h_s, a_s, gp_s, dh_s):
         def fetch(i, slot):
@@ -271,12 +276,12 @@
 
         def tile(i):
             slot = lax.rem(i, 2)
-            if behind:
+            if behind > 0:
                 @pl.when(i > 0)
                 def _():
                     forward(PARTS * i - 1)
             else:
-                forward(PARTS * i)
+                forward(PARTS * i + 1)
             for c in fetch(i, slot):
                 c.wait()
 
@@ -329,8 +334,13 @@
                     k = dinv * (inv * inv * inv) * (-1.0 / d)
                     dh_s[...] = (g.astype(f32) + du * inv + h * k).astype(bf16)
 
-            loop(0, layers - 1, lambda q: bwd(layers - 1 - q, False))
-            bwd(0, True)
+            shared = 0 if first or last else 1
+            loop(0, layers - 1 + shared, lambda q: bwd(layers - 1 - q, False))
+            if not shared:
+                @pl.when(i == tiles - 1)
+                def _():
+                    forward(PARTS * tiles - 1)
+                bwd(0, True)
 
         loop(0, tiles, tile)
 
@@ -340,7 +350,6 @@
     sent = tiles * PARTS - behind
 
     if first or last:
-        forward(sent)
         sent += 1
 
         def keep_gradient(og):

time: 1400 us -> 1370 us (0.979)
  Pallas kernels: 1400 us -> 1370 us
    pallas_call x4, Pallas kernels: 1350 us -> 1330 us  [run_step(): pl.pallas_call(functools.partial(step_kernel, step, steps, names), out_sh...]
where the time goes in v3:
time: 1370 us
  Pallas kernels  1370 us (100%)
    pallas_call x4, Pallas kernels, run_step(): pl.pallas_call(functools.partial(step_kernel, step, steps, names), out_sh...  1330 us
    pallas_call x1, Pallas kernels, finish(): pl.pallas_call(final_kernel, out_shape=(w_in, w_out, w_in, w_out), in_spe...  43.2 us

profile of v3, /device:TPU:0, one launch (start us, length us, event | category | flops | bytes accessed | tf_op | source)
XLA Modules:
  0.0 1371.8 jit_solution(7476537654171324891)
XLA Ops:
  0.6 234.6 %step0.1 = (bf16[1,4,8,384,1536]{4,3,2,1,0:T(8,128)(2,1)}, bf16[8,384,1536]{2,1,0:T(8,128)(2,1)}) custom-call(bf16[4,4096,384]{2,1,0:T(8,128)(2,1)} %bitcast.8, bf16[4,4096,384]{2,1,0:T(8,128)(2,1)} %bitcast.12, f32[4,384,1536]{2,1,0:T(8,128)} %bitcast.16, f32[4,1536,384]{2,1,0:T(8,128)} %bitcast.18), custom_call_target="tpu_custom_call" | custom-call | tf_op jit(solution)/shard_map/step0/pallas_call | solution.py:466
  235.3 429.9 %step1.1 = (bf16[2,4,8,384,1536]{4,3,2,1,0:T(8,128)(2,1)}, bf16[8,384,1536]{2,1,0:T(8,128)(2,1)}, f32[8,384,1536]{2,1,0:T(8,128)}, f32[8,384,1536]{2,1,0:T(8,128)}, bf16[8,384,1536]{2,1,0:T(8,128)(2,1)}) custom-call(bf16[4,4096,384]{2,1,0:T(8,128)(2,1)} %bitcast.9, bf16[4,4096,384]{2,1,0:T(8,128)(2,1)} %bitcast.13, f32[4,384,1536]{2,1,0:T(8,128)} %bitcast.17, ...), custom_call_target="tpu_custom_call" | custom-call | tf_op jit(solution)/shard_map/step1/pallas_call | solution.py:466
  665.1 439.0 %step2.1 = (bf16[2,4,8,384,1536]{4,3,2,1,0:T(8,128)(2,1)}, bf16[8,384,1536]{2,1,0:T(8,128)(2,1)}, f32[8,384,1536]{2,1,0:T(8,128)}, f32[8,384,1536]{2,1,0:T(8,128...) custom-call(bf16[4,4096,384]{2,1,0:T(8,128)(2,1)} %bitcast.10, ...), custom_call_target="tpu_custom_call" | custom-call | tf_op jit(solution)/shard_map/step2/pallas_call | solution.py:466
  1104.2 224.2 %step3.1 = (bf16[1,4,8,384,1536]{4,3,2,1,0:T(8,128)(2,1)}, bf16[8,384,1536]{2,1,0:T(8,128)(2,1)}) custom-call(bf16[4,4096,384]{2,1,0:T(8,128)(2,1)} %bitcast.11, bf16[4,4096,384]{2,1,0:T(8,128)(2,1)} %bitcast.15, bf16[8,384,1536]{2,1,0:T(8,128)(2,1)} %get-tuple-element.31.refs_2_, bf16[8,384,1536]{2,1,0:T(8,128)(2,1)} %get-tuple-element.32.refs_3_), custom_call_target="tpu_custom_call" | custom-call | tf_op jit(solution)/shard_map/step3/pallas_call | solution.py:466
  1328.4 43.2 %finish.1 = (f32[4,384,1536]{2,1,0:T(8,128)}, f32[4,1536,384]{2,1,0:T(8,128)}, f32[4,384,1536]{2,1,0:T(8,128)}, f32[4,1536,384]{2,1,0:T(8,128)}) custom-call(f32[8,384,1536]{2,1,0:T(8,128)} %get-tuple-element.29.p, f32[8,384,1536]{2,1,0:T(8,128)} %get-tuple-element.30.y, bf16[1,4,8,384,1536]{4,3,2,1,0:T(8,128)(2,1)} %get-tuple-element.33.nb, ...), custom_call_target="tpu_custom_call" | custom-call | tf_op jit(solution)/shard_map/finish/pallas_call | solution.py:483
